TPU v7x, 8 devices: a whole 2x2x1 slice. The times are simulated.
8 devices in a mesh: dp: 1 (over z), tp: 8 (over x, y, core).
Axes of the slice: x: 2, y: 2, z: 1, core: 2. Of those that a mesh axis runs over, the one named last changes fastest.
Arguments:
- x: bfloat16 [2048, 4096], P(('dp', 'tp'))
- w_gate: bfloat16 [4096, 14336], P(None, 'tp')
- w_up: bfloat16 [4096, 14336], P(None, 'tp')
- w_down: bfloat16 [14336, 4096], P('tp')
Outputs:
- output: bfloat16 [2048, 4096], P(('dp', 'tp'))
All inputs are finite; a program needn't handle non-finite values.
Results may differ from a plain program's by a relative error of at most 0.016.
Values are sent between devices in bfloat16 or wider.
A program may use at most 2 GiB of HBM per device.

v0:
```python
import jax
import jax.numpy as jnp
from jax import lax
from jax.sharding import PartitionSpec as P


def solution(mesh):
    def step(x, w_gate, w_up, w_down):
        rows = lax.all_gather(x, "tp", axis=0, tiled=True)
        gate = jnp.dot(rows, w_gate, preferred_element_type=jnp.float32)
        up = jnp.dot(rows, w_up, preferred_element_type=jnp.float32)
        hidden = (jax.nn.silu(gate) * up).astype(jnp.bfloat16)
        term = jnp.dot(hidden, w_down, preferred_element_type=jnp.float32).astype(jnp.bfloat16)
        return lax.psum_scatter(term, "tp", scatter_dimension=0, tiled=True)

    return jax.shard_map(
        step,
        mesh=mesh,
        in_specs=(P(("dp", "tp"), None), P(None, "tp"), P(None, "tp"), P("tp", None)),
        out_specs=P(("dp", "tp"), None),
        check_vma=False,
    )
```

profile of v0, /device:TPU:0, one launch (start us, length us, event | category | flops | bytes accessed | tf_op | source)
XLA Modules:
  0.0 323.6 jit_solution(16734685080214235653)
XLA Ops:
  6.5 0.0 all-gather.2.cloned.1.call-start
  6.5 0.7 all-gather.2.cloned.1.call-update
  7.3 0.0 reduce-scatter.2.cloned.1.call-start
  7.3 88.8 %all-gather.2.cloned.1.call-done = bf16[2048,4096]{1,0:T(8,128)(2,1)} async-done(((bf16[256,4096]{1,0:T(8,128)(2,1)}), bf16[2048,4096]{1,0:T(8,128)(2,1)}) %all-gather.2.cloned.1.call-update) | async-done | bytes 16777232 | tf_op jit(solution)/shard_map/all_gather | solution.py:9
  96.1 39.3 %fusion = f32[2048,1792]{1,0:T(8,128)} fusion(bf16[2048,4096]{1,0:T(8,128)(2,1)} %all-gather.2.cloned.1.call-done, bf16[4096,1792]{1,0:T(8,128)(2,1)} %param.5), kind=kOutput, calls=%fused_computation.2 | convolution fusion | flops 30064771072 | bytes 46137344 | tf_op jit(solution)/shard_map/dot_general | solution.py:10
  135.4 38.9 %multiply_convert_fusion = bf16[2048,1792]{1,0:T(8,128)(2,1)S(1)} fusion(f32[2048,1792]{1,0:T(8,128)} %fusion, bf16[2048,4096]{1,0:T(8,128)(2,1)} %all-gather.2.cloned.1.call-done, bf16[4096,1792]{1,0:T(8,128)(2,1)} %param.6), kind=kOutput, calls=%fused_computation.1 | convolution fusion | flops 30086791168 | bytes 53477376 | tf_op jit(solution)/shard_map/dot_general | solution.py:11
  174.3 35.4 %convolution_convert_fusion = bf16[2048,4096]{1,0:T(8,128)(2,1)} fusion(bf16[2048,1792]{1,0:T(8,128)(2,1)S(1)} %multiply_convert_fusion, bf16[1792,4096]{1,0:T(8,128)(2,1)} %param.7), kind=kOutput, calls=%fused_computation | convolution fusion | flops 30073159680 | bytes 38797312 | tf_op jit(solution)/shard_map/dot_general | solution.py:13
  209.7 0.0 reduce-scatter.2.cloned.1.call-update
  209.7 107.1 %reduce-scatter.2.cloned.1.call-done = bf16[256,4096]{1,0:T(8,128)(2,1)} async-done(((bf16[2048,4096]{1,0:T(8,128)(2,1)}), bf16[256,4096]{1,0:T(8,128)(2,1)}) %reduce-scatter.2.cloned.1.call-update) | async-done | bytes 2097168 | tf_op jit(solution)/shard_map/reduce_scatter | solution.py:14
Async XLA Ops:
  6.5 89.6 %all-gather.2.cloned.1.call-start = ((), (), s32[]{:S(2)}) async-start(), calls=%async_computation.1 | async-start | bytes 18874368 | tf_op jit(solution)/shard_map/all_gather | solution.py:9
  7.3 309.5 %reduce-scatter.2.cloned.1.call-start = ((), (), s32[]{:S(2)}) async-start(), calls=%async_computation.2 | async-start | bytes 18874368 | tf_op jit(solution)/shard_map/reduce_scatter | solution.py:14
Sparse Core Ops, SparseCore 0:
  9.1 86.8 all-gather.1
  209.8 106.9 reduce-scatter.1
where the time goes:
time: 324 us
  waiting for transfers between devices  197 us (61%)
  matrix products  114 us (35%)
  between operations  13.4 us (4%)
    reduce_scatter x1, waiting for transfers between devices, step(): return lax.psum_scatter(term, 'tp', scatter_dimension=0, tiled=True)  107 us
    all_gather x1, waiting for transfers between devices, step(): rows = lax.all_gather(x, 'tp', axis=0, tiled=True)  88.8 us
    dot_general x1, matrix products, step(): gate = jnp.dot(rows, w_gate, preferred_element_type=jnp.float32)  39.3 us
    dot_general x1, matrix products, step(): up = jnp.dot(rows, w_up, preferred_element_type=jnp.float32)  38.9 us
    dot_general x1, matrix products, step(): jnp.dot(hidden, w_down, preferred_element_type=jnp.float32)  35.4 us
  transfers between devices with their start and end apart: 2, of which 2 were waited for; matrix products, arithmetic and copies ran while one was open for 0% of the time, Pallas kernels for 0%

commit v1 on v0

v1 whole, which is shorter than its diff:
```python
import jax
import jax.numpy as jnp
from jax import lax
from jax.experimental import pallas as pl
from jax.experimental.pallas import tpu as pltpu
from jax.sharding import PartitionSpec as P

F32 = jnp.float32
BF16 = jnp.bfloat16
MESH = pl.DeviceIdType.MESH

SIB, YN, XN = 1, 2, 4
LINK = (XN, YN)
OWN, FX, FY, DG = 0, 1, 2, 3
PIECE = 64
STEPS = 8
GT = 256
DT = 1024


def body(
    x, wg_h, wu_h, wd_h, y, xg, fh,
    wg, wu, wd, xb, hb, mine, tsend, trecv, outd, outg, rly, hold, fv,
    so, ro, sr, rr, ss, rs, st, rt, sd, rd, sg, rg, sq, rq, lx, lw, lf, ly,
):
    me = lax.axis_index("tp")
    d = x.shape[1]
    half = d // 2
    ff = wg.shape[1]
    cols = (pl.ds(0, half), pl.ds(half, half))

    def remote(src, dst, send, recv, mask):
        return pltpu.make_async_remote_copy(
            src_ref=src, dst_ref=dst, send_sem=send, recv_sem=recv,
            device_id={"tp": me ^ mask}, device_id_type=MESH,
        )

    def rows(k, n=1):
        return pl.ds(k * PIECE, n * PIECE)

    def own(l, k):
        return remote(x.at[rows(k)], xg.at[FX + l, 0, rows(k)], so.at[l, k], ro.at[l, k], LINK[l])

    def relay(l, r):
        src = xg.at[FY - l, 0, rows(2 * r + l)]
        return remote(src, xg.at[DG, 0, rows(2 * r + l)], sr.at[l, r], rr.at[l, r], LINK[l])

    def hand(b, k):
        if b == OWN:
            return remote(x, xg.at[OWN, 1], ss.at[0, 0], rs.at[0, 0], SIB)
        return remote(xg.at[b, 0, rows(k)], xg.at[b, 1, rows(k)], ss.at[b, k], rs.at[b, k], SIB)

    def term(s):
        slot = s % 2
        return remote(tsend, trecv.at[slot], st.at[slot], rt.at[slot], SIB)

    def landing(l, k):
        return fh.at[l, k] if k < 2 else fv.at[l, k - 2]

    def direct(l, k):
        return remote(
            outd.at[k, rows(l)], landing(l, k).at[:, cols[l]], sd.at[l, k], rd.at[l, k], LINK[l]
        )

    def diag(l, c):
        return remote(outg.at[c, :, cols[l]], rly.at[c, l], sg.at[l, c], rg.at[l, c], LINK[l])

    def relayed(l, k):
        src = rly.at[k // 2, 1 - l, rows(k % 2)]
        return remote(src, landing(l, k).at[:, cols[1 - l]], sq.at[l, k], rq.at[l, k], LINK[l])

    def pieces(s):
        if s < 4:
            return ((FX, s), (FY, s))
        b, c = (DG, s - 4) if s < 6 else (OWN, s - 6)
        return ((b, 2 * c), (b, 2 * c + 1))

    def load(s, side):
        out = []
        for i, (b, k) in enumerate(pieces(s)):
            src = x.at[rows(k)] if (b == OWN and side == 0) else xg.at[b, side, rows(k)]
            out.append(pltpu.make_async_copy(src, xb.at[rows(2 * side + i)], lx.at[side, i]))
        return out

    def take(s):
        if s < 4:
            for l in range(2):
                own(l, s).wait_recv()
        elif s < 6:
            for l in range(2):
                relay(l, s - 4).wait_recv()
        if s < 6:
            for b, k in pieces(s):
                hand(b, k).start()
        for c in load(s, 0):
            c.start()
        if s == 1:
            for l in range(2):
                relay(l, 0).start()
        if s == 3:
            for l in range(2):
                relay(l, 1).start()

    def take_other(s):
        if s < 6:
            for b, k in pieces(s):
                hand(b, k).wait_recv()
        elif s == 6:
            hand(OWN, 0).wait_recv()
        for c in load(s, 1):
            c.start()

    weights = [
        pltpu.make_async_copy(h, v, lw.at[i])
        for i, (h, v) in enumerate(((wg_h, wg), (wu_h, wu), (wd_h, wd)))
    ]

    def total(r, slot):
        return mine[r] + trecv[slot, r].astype(F32)

    def blocks(n, f):
        def one(i, carry):
            f(pl.multiple_of(i * 16, 16))
            return carry

        lax.fori_loop(0, n, one, 0)

    def settle(p):
        slot = p % 2
        term(p).wait_recv()
        if p < 4:
            for l in range(2):

                def f(i, l=l):
                    r = pl.ds(l * PIECE + i, 16)
                    v = total(r, slot)
                    a, b = v[:, :half], v[:, half:]
                    outd[p, r] = (b if l else a).astype(BF16)
                    hold[p, r] = a if l else b

                blocks(PIECE // 16, f)
                direct(l, p).start()
        elif p < 6:

            def f(i):
                r = pl.ds(i, 16)
                outg[p - 4, r] = total(r, slot).astype(BF16)

            blocks(8, f)
            for l in range(2):
                diag(l, p - 4).start()
        else:

            def f(i):
                r = pl.ds(i, 16)
                v = total(r, slot)
                hold[0, r] = v[:, :half]
                hold[1, r] = v[:, half:]

            blocks(8, f)

    def pass_on(c):
        for l in range(2):
            diag(1 - l, c).wait_recv()
        for k in (2 * c, 2 * c + 1):
            for l in range(2):

                def f(i, k=k, l=l):
                    r = pl.ds((k % 2) * PIECE + i, 16)
                    v = hold[k, pl.ds(l * PIECE + i, 16)] + rly[c, 1 - l, r].astype(F32)
                    rly[c, 1 - l, r] = v.astype(BF16)

                blocks(PIECE // 16, f)
                relayed(l, k).start()

    def gate_up(lo, hi):
        def one(j, carry):
            c = pl.ds(pl.multiple_of(j * GT, GT), GT)
            g = jnp.dot(xb[...], wg[:, c], preferred_element_type=F32)
            u = jnp.dot(xb[...], wu[:, c], preferred_element_type=F32)
            hb[:, c] = (jax.nn.silu(g) * u).astype(BF16)
            return carry

        lax.fori_loop(lo, hi, one, 0)

    def down(lo, hi):
        def one(j, carry):
            c = pl.ds(pl.multiple_of(j * DT, DT), DT)
            t = jnp.dot(hb[...], wd[:, c], preferred_element_type=F32)
            mine[:, c] = t[: 2 * PIECE]
            tsend[:, c] = t[2 * PIECE :].astype(BF16)
            return carry

        lax.fori_loop(lo, hi, one, 0)

    barrier = pltpu.get_barrier_semaphore()
    for mask in (SIB, YN, XN):
        pl.semaphore_signal(barrier, inc=1, device_id={"tp": me ^ mask}, device_id_type=MESH)
    pl.semaphore_wait(barrier, 3)

    for k in range(4):
        for l in range(2):
            own(l, k).start()
    for w in weights:
        w.start()
    take(0)
    take_other(0)
    hand(OWN, 0).start()
    weights[0].wait()
    weights[1].wait()

    def at(s, table):
        for k, fs in table.items():

            @pl.when(s == k)
            def _(fs=fs):
                for f, *args in fs:
                    f(*args)

    after_tiles = {p + 1: [(settle, p)] for p in range(7)}
    after_gate = {s: [(take, s + 1)] for s in range(7)}
    after_gate[0].append((weights[2].wait,))
    after_gate[6].append((pass_on, 0))
    after_gate[7] = [(pass_on, 1)]
    for s in range(1, STEPS):
        after_gate[s].append((term(s - 1).wait_send,))
    late = {s: [(take_other, s + 1)] for s in range(7)}
    ends = {s: [(term(s).start,)] for s in range(STEPS)}

    def step(s, carry):
        for side in range(2):
            for c in load(0, side):
                c.wait()
        gate_up(0, 3)
        at(s, after_tiles)
        gate_up(3, ff // GT)
        at(s, after_gate)
        down(0, d // DT - 1)
        at(s, late)
        down(d // DT - 1, d // DT)
        at(s, ends)
        return carry

    lax.fori_loop(0, STEPS, step, 0)

    for k in range(2):
        for l in range(2):
            direct(l, k).wait_recv()
            relayed(l, k).wait_recv()
    back = [
        pltpu.make_async_copy(fh.at[l, k], xb.at[rows(2 * l + k)], lf.at[l, k])
        for l in range(2)
        for k in range(2)
    ]
    for c in back:
        c.start()
    term(7).wait_recv()
    for k in range(4):
        for l in range(2):
            direct(l, k).wait_send()
    for c in back:
        c.wait()

    def first(i):
        r = pl.ds(i, 16)
        v = xb[r].astype(F32) + xb[pl.ds(128 + i, 16)].astype(F32)
        outd[0, r] = (hold[0, r] + v[:, :half]).astype(BF16)
        outd[1, r] = (hold[1, r] + v[:, half:]).astype(BF16)

    blocks(8, first)
    outs = [
        pltpu.make_async_copy(outd.at[h], y.at[rows(0, 2), cols[h]], ly.at[0, h]) for h in range(2)
    ]
    for c in outs:
        c.start()
    for k in (2, 3):
        for l in range(2):
            direct(l, k).wait_recv()
            relayed(l, k).wait_recv()

        def last(i, k=k):
            r = pl.ds((k - 2) * PIECE + i, 16)
            q = pl.ds(i, 16)
            v = total(r, 1) + fv[0, k - 2, q].astype(F32) + fv[1, k - 2, q].astype(F32)
            outd[2, r] = v[:, :half].astype(BF16)
            outd[3, r] = v[:, half:].astype(BF16)

        blocks(PIECE // 16, last)
        for h in range(2):
            c = pltpu.make_async_copy(
                outd.at[2 + h, rows(k - 2)], y.at[rows(k), cols[h]], ly.at[k - 1, h]
            )
            c.start()
            outs.append(c)
    for c in outs:
        c.wait()
    term(7).wait_send()
    hand(OWN, 0).wait_send()
    for l in range(2):
        for k in range(4):
            own(l, k).wait_send()
            relayed(l, k).wait_send()
        for r in range(2):
            relay(l, r).wait_send()
            diag(l, r).wait_send()
    for b in (FX, FY, DG):
        for k in range(4):
            hand(b, k).wait_send()


def solution(mesh):
    def step(x, w_gate, w_up, w_down):
        r, d = x.shape
        ff = w_gate.shape[1]
        hbm = pl.BlockSpec(memory_space=pl.ANY)
        dma = pltpu.SemaphoreType.DMA
        half = d // 2
        y, _, _ = pl.pallas_call(
            body,
            out_shape=(
                jax.ShapeDtypeStruct((r, d), BF16),
                jax.ShapeDtypeStruct((4, 2, r, d), BF16),
                jax.ShapeDtypeStruct((2, 2, PIECE, d), BF16),
            ),
            in_specs=[hbm] * 4,
            out_specs=(hbm,) * 3,
            scratch_shapes=[
                pltpu.VMEM((d, ff), BF16),
                pltpu.VMEM((d, ff), BF16),
                pltpu.VMEM((ff, d), BF16),
                pltpu.VMEM((256, d), BF16),
                pltpu.VMEM((256, ff), BF16),
                pltpu.VMEM((128, d), F32),
                pltpu.VMEM((128, d), BF16),
                pltpu.VMEM((2, 128, d), BF16),
                pltpu.VMEM((4, 128, half), BF16),
                pltpu.VMEM((2, 128, d), BF16),
                pltpu.VMEM((2, 2, 128, half), BF16),
                pltpu.VMEM((4, 128, half), F32),
                pltpu.VMEM((2, 2, PIECE, d), BF16),
                dma((2, 4)), dma((2, 4)), dma((2, 2)), dma((2, 2)), dma((4, 4)), dma((4, 4)),
                dma((2,)), dma((2,)), dma((2, 4)), dma((2, 4)), dma((2, 2)), dma((2, 2)),
                dma((2, 4)), dma((2, 4)), dma((2, 2)), dma((3,)), dma((2, 2)), dma((3, 2)),
            ],
            compiler_params=pltpu.CompilerParams(
                collective_id=0, has_side_effects=True, vmem_limit_bytes=67043328
            ),
            cost_estimate=pl.CostEstimate(
                flops=6 * 8 * r * d * ff, bytes_accessed=6 * d * ff + 4 * r * d, transcendentals=8 * r * ff
            ),
            name="mlp",
        )(x, w_gate, w_up, w_down)
        return y

    return jax.shard_map(
        step,
        mesh=mesh,
        in_specs=(P(("dp", "tp"), None), P(None, "tp"), P(None, "tp"), P("tp", None)),
        out_specs=P(("dp", "tp"), None),
        check_vma=False,
    )
```

time: 324 us -> 149 us (0.46)
  waiting for transfers between devices: 197 us -> 0 us
  Pallas kernels: 0 us -> 145 us
  matrix products: 114 us -> 0 us
  between operations: 13.4 us -> 0.01 us
    pallas_call x0 -> x1, Pallas kernels: none -> 145 us  [step(): pl.pallas_call(body, out_shape=(jax.ShapeDtypeStruct((r, d), BF16), jax.S...]
    dot_general x3 -> x0, matrix products: 114 us -> none  [the longest x1 39.3 us: step(): gate = jnp.dot(rows, w_gate, preferred_element_type=jnp.float32)]
    reduce_scatter x1 -> x0, waiting for transfers between devices: 107 us -> none  [step(): return lax.psum_scatter(term, 'tp', scatter_dimension=0, tiled=True)]
    all_gather x1 -> x0, waiting for transfers between devices: 88.8 us -> none  [step(): rows = lax.all_gather(x, 'tp', axis=0, tiled=True)]
  transfers between devices with their start and end apart: 2 -> 0, of which waited for: 2 -> 0; matrix products, arithmetic and copies ran while one was open for 0% -> 0% of each run, Pallas kernels for 0% -> 0%
where the time goes in v1:
time: 149 us; the launch traced here: 148 us
  Pallas kernels  145 us (97%)
  local copies, waits for them, and re-layouts  3.13 us (2%)
    pallas_call x1, Pallas kernels, step(): pl.pallas_call(body, out_shape=(jax.ShapeDtypeStruct((r, d), BF16), jax.S...  145 us
    unnamed x1, local copies, waits for them, and re-layouts  3.13 us

profile of v1, /device:TPU:0, one launch (start us, length us, event | category | flops | bytes accessed | tf_op | source)
XLA Modules:
  0.0 148.2 jit_solution(515902680155176287)
XLA Ops:
  0.0 145.1 %mlp.1 = (bf16[256,4096]{1,0:T(8,128)(2,1)}, bf16[4,2,256,4096]{3,2,1,0:T(8,128)(2,1)}, bf16[2,2,64,4096]{3,2,1,0:T(8,128)(2,1)}) custom-call(bf16[256,4096]{1,0:T(8,128)(2,1)} %x.1, bf16[4096,1792]{1,0:T(8,128)(2,1)} %wg_h.1, bf16[4096,1792]{1,0:T(8,128)(2,1)} %wu_h.1, bf16[1792,4096]{1,0:T(8,128)(2,1)} %wd_h.1), custom_call_target="tpu_custom_call" | custom-call | flops 90194313216 | bytes 48234496 | tf_op jit(solution)/shard_map/mlp/pallas_call | solution.py:318
  145.1 3.1 %copy.6 = bf16[256,4096]{1,0:T(8,128)(2,1)} copy(bf16[256,4096]{1,0:T(8,128)(2,1)} %get-tuple-element.6) | data formatting | bytes 4194304

commit v2 on v1

--- a/solution.py
+++ b/solution.py
@@ -14,6 +14,9 @@
 OWN, FX, FY, DG = 0, 1, 2, 3
 PIECE = 64
 STEPS = 8
+X_STEPS = {0: 0, 1: 1, 2: 2, 5: 3}
+D_STEPS = {3: 0, 4: 1}
+SWAP = (1, 0, 3, 2)
 GT = 256
 DT = 1024
 
@@ -38,12 +41,17 @@
     def rows(k, n=1):
         return pl.ds(k * PIECE, n * PIECE)
 
+    def turn(l, k):
+        return SWAP[k] if l else k
+
     def own(l, k):
         return remote(x.at[rows(k)], xg.at[FX + l, 0, rows(k)], so.at[l, k], ro.at[l, k], LINK[l])
 
     def relay(l, r):
-        src = xg.at[FY - l, 0, rows(2 * r + l)]
-        return remote(src, xg.at[DG, 0, rows(2 * r + l)], sr.at[l, r], rr.at[l, r], LINK[l])
+        k = 2 * r + 1 - l
+        return remote(
+            xg.at[FY - l, 0, rows(k)], xg.at[DG, 0, rows(k)], sr.at[l, r], rr.at[l, r], LINK[l]
+        )
 
     def hand(b, k):
         if b == OWN:
@@ -59,7 +67,7 @@
 
     def direct(l, k):
         return remote(
-            outd.at[k, rows(l)], landing(l, k).at[:, cols[l]], sd.at[l, k], rd.at[l, k], LINK[l]
+            outd.at[turn(l, k), rows(l)], landing(l, k).at[:, cols[l]], sd.at[l, k], rd.at[l, k], LINK[l]
         )
 
     def diag(l, c):
@@ -70,9 +78,9 @@
         return remote(src, landing(l, k).at[:, cols[1 - l]], sq.at[l, k], rq.at[l, k], LINK[l])
 
     def pieces(s):
-        if s < 4:
-            return ((FX, s), (FY, s))
-        b, c = (DG, s - 4) if s < 6 else (OWN, s - 6)
+        if s in X_STEPS:
+            return tuple((FX + l, turn(l, X_STEPS[s])) for l in range(2))
+        b, c = (DG, D_STEPS[s]) if s in D_STEPS else (OWN, s - 6)
         return ((b, 2 * c), (b, 2 * c + 1))
 
     def load(s, side):
@@ -83,12 +91,12 @@
         return out
 
     def take(s):
-        if s < 4:
-            for l in range(2):
-                own(l, s).wait_recv()
-        elif s < 6:
-            for l in range(2):
-                relay(l, s - 4).wait_recv()
+        if s in X_STEPS:
+            for l in range(2):
+                own(l, turn(l, X_STEPS[s])).wait_recv()
+        elif s in D_STEPS:
+            for l in range(2):
+                relay(l, D_STEPS[s]).wait_recv()
         if s < 6:
             for b, k in pieces(s):
                 hand(b, k).start()
@@ -97,9 +105,11 @@
         if s == 1:
             for l in range(2):
                 relay(l, 0).start()
-        if s == 3:
+                own(l, turn(l, 3)).start()
+        if s == 2:
             for l in range(2):
                 relay(l, 1).start()
+                direct(l, turn(l, 0)).start()
 
     def take_other(s):
         if s < 6:
@@ -128,27 +138,30 @@
     def settle(p):
         slot = p % 2
         term(p).wait_recv()
-        if p < 4:
+        if p in X_STEPS:
+            n = X_STEPS[p]
             for l in range(2):
 
                 def f(i, l=l):
                     r = pl.ds(l * PIECE + i, 16)
                     v = total(r, slot)
                     a, b = v[:, :half], v[:, half:]
-                    outd[p, r] = (b if l else a).astype(BF16)
-                    hold[p, r] = a if l else b
+                    outd[n, r] = (b if l else a).astype(BF16)
+                    hold[n, r] = a if l else b
 
                 blocks(PIECE // 16, f)
-                direct(l, p).start()
-        elif p < 6:
+                if n > 0:
+                    direct(l, turn(l, n)).start()
+        elif p in D_STEPS:
+            n = D_STEPS[p]
 
             def f(i):
                 r = pl.ds(i, 16)
-                outg[p - 4, r] = total(r, slot).astype(BF16)
+                outg[n, r] = total(r, slot).astype(BF16)
 
             blocks(8, f)
             for l in range(2):
-                diag(l, p - 4).start()
+                diag(l, n).start()
         else:
 
             def f(i):
@@ -167,7 +180,7 @@
 
                 def f(i, k=k, l=l):
                     r = pl.ds((k % 2) * PIECE + i, 16)
-                    v = hold[k, pl.ds(l * PIECE + i, 16)] + rly[c, 1 - l, r].astype(F32)
+                    v = hold[turn(l, k), pl.ds(l * PIECE + i, 16)] + rly[c, 1 - l, r].astype(F32)
                     rly[c, 1 - l, r] = v.astype(BF16)
 
                 blocks(PIECE // 16, f)
@@ -198,16 +211,17 @@
         pl.semaphore_signal(barrier, inc=1, device_id={"tp": me ^ mask}, device_id_type=MESH)
     pl.semaphore_wait(barrier, 3)
 
-    for k in range(4):
-        for l in range(2):
-            own(l, k).start()
-    for w in weights:
-        w.start()
+    for k in range(3):
+        for l in range(2):
+            own(l, turn(l, k)).start()
+    for i in range(2):
+        weights[i].start()
+    for i in range(2):
+        weights[i].wait()
+    weights[2].start()
     take(0)
     take_other(0)
     hand(OWN, 0).start()
-    weights[0].wait()
-    weights[1].wait()
 
     def at(s, table):
         for k, fs in table.items():
@@ -219,13 +233,16 @@
 
     after_tiles = {p + 1: [(settle, p)] for p in range(7)}
     after_gate = {s: [(take, s + 1)] for s in range(7)}
+    late = {s: [(take_other, s + 1)] for s in range(7)}
+    ends = {s: [(term(s).start,)] for s in range(STEPS)}
+    ends[3] += after_gate.pop(3) + late.pop(3)
+    after_gate.setdefault(3, [])
+    after_gate[7] = []
     after_gate[0].append((weights[2].wait,))
-    after_gate[6].append((pass_on, 0))
-    after_gate[7] = [(pass_on, 1)]
+    after_gate[5].append((pass_on, 0))
+    ends[6].append((pass_on, 1))
     for s in range(1, STEPS):
         after_gate[s].append((term(s - 1).wait_send,))
-    late = {s: [(take_other, s + 1)] for s in range(7)}
-    ends = {s: [(term(s).start,)] for s in range(STEPS)}
 
     def step(s, carry):
         for side in range(2):

time: 149 us -> 146 us (0.980)
  Pallas kernels: 145 us -> 142 us
    pallas_call x1, Pallas kernels: 145 us -> 142 us  [step(): pl.pallas_call(body, out_shape=(jax.ShapeDtypeStruct((r, d), BF16), jax.S...]
where the time goes in v2:
time: 146 us; the launch traced here: 145 us
  Pallas kernels  142 us (97%)
  local copies, waits for them, and re-layouts  3.13 us (2%)
    pallas_call x1, Pallas kernels, step(): pl.pallas_call(body, out_shape=(jax.ShapeDtypeStruct((r, d), BF16), jax.S...  142 us
    unnamed x1, local copies, waits for them, and re-layouts  3.13 us

profile of v2, /device:TPU:0, one launch (start us, length us, event | category | flops | bytes accessed | tf_op | source)
XLA Modules:
  0.0 145.4 jit_solution(13281347142557625536)
XLA Ops:
  0.0 142.3 %mlp.1 = (bf16[256,4096]{1,0:T(8,128)(2,1)}, bf16[4,2,256,4096]{3,2,1,0:T(8,128)(2,1)}, bf16[2,2,64,4096]{3,2,1,0:T(8,128)(2,1)}) custom-call(bf16[256,4096]{1,0:T(8,128)(2,1)} %x.1, bf16[4096,1792]{1,0:T(8,128)(2,1)} %wg_h.1, bf16[4096,1792]{1,0:T(8,128)(2,1)} %wu_h.1, bf16[1792,4096]{1,0:T(8,128)(2,1)} %wd_h.1), custom_call_target="tpu_custom_call" | custom-call | flops 90194313216 | bytes 48234496 | tf_op jit(solution)/shard_map/mlp/pallas_call | solution.py:335
  142.3 3.1 %copy.6 = bf16[256,4096]{1,0:T(8,128)(2,1)} copy(bf16[256,4096]{1,0:T(8,128)(2,1)} %get-tuple-element.6) | data formatting | bytes 4194304

commit v3 on v2

--- a/solution.py
+++ b/solution.py
@@ -14,8 +14,8 @@
 OWN, FX, FY, DG = 0, 1, 2, 3
 PIECE = 64
 STEPS = 8
-X_STEPS = {0: 0, 1: 1, 2: 2, 5: 3}
-D_STEPS = {3: 0, 4: 1}
+X_STEPS = {0: 0, 1: 1, 2: 2, 4: 3}
+D_STEPS = {3: 0, 5: 1}
 SWAP = (1, 0, 3, 2)
 GT = 256
 DT = 1024
@@ -194,7 +194,7 @@
             hb[:, c] = (jax.nn.silu(g) * u).astype(BF16)
             return carry
 
-        lax.fori_loop(lo, hi, one, 0)
+        lax.fori_loop(lo, hi, one, 0, unroll=True)
 
     def down(lo, hi):
         def one(j, carry):
@@ -204,7 +204,7 @@
             tsend[:, c] = t[2 * PIECE :].astype(BF16)
             return carry
 
-        lax.fori_loop(lo, hi, one, 0)
+        lax.fori_loop(lo, hi, one, 0, unroll=True)
 
     barrier = pltpu.get_barrier_semaphore()
     for mask in (SIB, YN, XN):
@@ -235,12 +235,10 @@
     after_gate = {s: [(take, s + 1)] for s in range(7)}
     late = {s: [(take_other, s + 1)] for s in range(7)}
     ends = {s: [(term(s).start,)] for s in range(STEPS)}
-    ends[3] += after_gate.pop(3) + late.pop(3)
-    after_gate.setdefault(3, [])
     after_gate[7] = []
     after_gate[0].append((weights[2].wait,))
-    after_gate[5].append((pass_on, 0))
-    ends[6].append((pass_on, 1))
+    after_gate[6].append((pass_on, 0))
+    ends[7].append((pass_on, 1))
     for s in range(1, STEPS):
         after_gate[s].append((term(s - 1).wait_send,))
 

time: 146 us -> 146 us (level)
  no operation moved by 1% of the time
where the time goes in v3:
time: 146 us; the launch traced here: 145 us
  Pallas kernels  142 us (97%)
  local copies, waits for them, and re-layouts  3.13 us (2%)
    pallas_call x1, Pallas kernels, step(): pl.pallas_call(body, out_shape=(jax.ShapeDtypeStruct((r, d), BF16), jax.S...  142 us
    unnamed x1, local copies, waits for them, and re-layouts  3.13 us

profile of v3, /device:TPU:0, one launch (start us, length us, event | category | flops | bytes accessed | tf_op | source)
XLA Modules:
  0.0 145.4 jit_solution(15064191156687963032)
XLA Ops:
  0.0 142.3 %mlp.1 = (bf16[256,4096]{1,0:T(8,128)(2,1)}, bf16[4,2,256,4096]{3,2,1,0:T(8,128)(2,1)}, bf16[2,2,64,4096]{3,2,1,0:T(8,128)(2,1)}) custom-call(bf16[256,4096]{1,0:T(8,128)(2,1)} %x.1, bf16[4096,1792]{1,0:T(8,128)(2,1)} %wg_h.1, bf16[4096,1792]{1,0:T(8,128)(2,1)} %wu_h.1, bf16[1792,4096]{1,0:T(8,128)(2,1)} %wd_h.1), custom_call_target="tpu_custom_call" | custom-call | flops 90194313216 | bytes 48234496 | tf_op jit(solution)/shard_map/mlp/pallas_call | solution.py:333
  142.3 3.1 %copy.6 = bf16[256,4096]{1,0:T(8,128)(2,1)} copy(bf16[256,4096]{1,0:T(8,128)(2,1)} %get-tuple-element.6) | data formatting | bytes 4194304

commit v4 on v3

--- a/solution.py
+++ b/solution.py
@@ -23,8 +23,8 @@
 
 def body(
     x, wg_h, wu_h, wd_h, y, xg, fh,
-    wg, wu, wd, xb, hb, mine, tsend, trecv, outd, outg, rly, hold, fv,
-    so, ro, sr, rr, ss, rs, st, rt, sd, rd, sg, rg, sq, rq, lx, lw, lf, ly,
+    wg, wu, wd, xb, hb, mine, tsend, trecv, outg, rly, hold, fv,
+    so, ro, sr, rr, ss, rs, st, rt, sd, rd, sg, rg, sq, rq, lx, lw, lf,
 ):
     me = lax.axis_index("tp")
     d = x.shape[1]
@@ -62,12 +62,12 @@
         slot = s % 2
         return remote(tsend, trecv.at[slot], st.at[slot], rt.at[slot], SIB)
 
-    def landing(l, k):
-        return fh.at[l, k] if k < 2 else fv.at[l, k - 2]
+    def landing(l, k, cols):
+        return fh.at[l, k, :, cols] if k < 2 else fv.at[l, k - 2, :, cols]
 
     def direct(l, k):
         return remote(
-            outd.at[turn(l, k), rows(l)], landing(l, k).at[:, cols[l]], sd.at[l, k], rd.at[l, k], LINK[l]
+            y.at[rows(2 * (turn(l, k) // 2) + l), cols[turn(l, k) % 2]], landing(l, k, cols[l]), sd.at[l, k], rd.at[l, k], LINK[l]
         )
 
     def diag(l, c):
@@ -75,7 +75,7 @@
 
     def relayed(l, k):
         src = rly.at[k // 2, 1 - l, rows(k % 2)]
-        return remote(src, landing(l, k).at[:, cols[1 - l]], sq.at[l, k], rq.at[l, k], LINK[l])
+        return remote(src, landing(l, k, cols[1 - l]), sq.at[l, k], rq.at[l, k], LINK[l])
 
     def pieces(s):
         if s in X_STEPS:
@@ -146,7 +146,8 @@
                     r = pl.ds(l * PIECE + i, 16)
                     v = total(r, slot)
                     a, b = v[:, :half], v[:, half:]
-                    outd[n, r] = (b if l else a).astype(BF16)
+                    q = pl.ds((n // 2) * 2 * PIECE + l * PIECE + i, 16)
+                    y[q, cols[n % 2]] = (b if l else a).astype(BF16)
                     hold[n, r] = a if l else b
 
                 blocks(PIECE // 16, f)
@@ -258,57 +259,42 @@
 
     lax.fori_loop(0, STEPS, step, 0)
 
+    for k in range(4):
+        for l in range(2):
+            direct(l, k).wait_send()
     for k in range(2):
         for l in range(2):
             direct(l, k).wait_recv()
             relayed(l, k).wait_recv()
-    back = [
-        pltpu.make_async_copy(fh.at[l, k], xb.at[rows(2 * l + k)], lf.at[l, k])
-        for l in range(2)
-        for k in range(2)
-    ]
-    for c in back:
-        c.start()
+        back = [
+            pltpu.make_async_copy(fh.at[l, k], xb.at[rows(2 * l + k)], lf.at[l, k])
+            for l in range(2)
+        ]
+        for c in back:
+            c.start()
+        for c in back:
+            c.wait()
+
+        def first(i, k=k):
+            r = pl.ds(k * PIECE + i, 16)
+            v = xb[r].astype(F32) + xb[pl.ds((2 + k) * PIECE + i, 16)].astype(F32)
+            y[r, cols[0]] = (hold[0, r] + v[:, :half]).astype(BF16)
+            y[r, cols[1]] = (hold[1, r] + v[:, half:]).astype(BF16)
+
+        blocks(PIECE // 16, first)
     term(7).wait_recv()
-    for k in range(4):
-        for l in range(2):
-            direct(l, k).wait_send()
-    for c in back:
-        c.wait()
-
-    def first(i):
-        r = pl.ds(i, 16)
-        v = xb[r].astype(F32) + xb[pl.ds(128 + i, 16)].astype(F32)
-        outd[0, r] = (hold[0, r] + v[:, :half]).astype(BF16)
-        outd[1, r] = (hold[1, r] + v[:, half:]).astype(BF16)
-
-    blocks(8, first)
-    outs = [
-        pltpu.make_async_copy(outd.at[h], y.at[rows(0, 2), cols[h]], ly.at[0, h]) for h in range(2)
-    ]
-    for c in outs:
-        c.start()
     for k in (2, 3):
         for l in range(2):
             direct(l, k).wait_recv()
             relayed(l, k).wait_recv()
 
         def last(i, k=k):
-            r = pl.ds((k - 2) * PIECE + i, 16)
             q = pl.ds(i, 16)
-            v = total(r, 1) + fv[0, k - 2, q].astype(F32) + fv[1, k - 2, q].astype(F32)
-            outd[2, r] = v[:, :half].astype(BF16)
-            outd[3, r] = v[:, half:].astype(BF16)
+            v = fv[0, k - 2, q].astype(F32) + fv[1, k - 2, q].astype(F32)
+            v = total(pl.ds((k - 2) * PIECE + i, 16), 1) + v
+            y[pl.ds(k * PIECE + i, 16)] = v.astype(BF16)
 
         blocks(PIECE // 16, last)
-        for h in range(2):
-            c = pltpu.make_async_copy(
-                outd.at[2 + h, rows(k - 2)], y.at[rows(k), cols[h]], ly.at[k - 1, h]
-            )
-            c.start()
-            outs.append(c)
-    for c in outs:
-        c.wait()
     term(7).wait_send()
     hand(OWN, 0).wait_send()
     for l in range(2):
@@ -333,12 +319,12 @@
         y, _, _ = pl.pallas_call(
             body,
             out_shape=(
-                jax.ShapeDtypeStruct((r, d), BF16),
+                pltpu.VMEM((r, d), BF16),
                 jax.ShapeDtypeStruct((4, 2, r, d), BF16),
                 jax.ShapeDtypeStruct((2, 2, PIECE, d), BF16),
             ),
             in_specs=[hbm] * 4,
-            out_specs=(hbm,) * 3,
+            out_specs=(pl.BlockSpec(memory_space=pltpu.VMEM), hbm, hbm),
             scratch_shapes=[
                 pltpu.VMEM((d, ff), BF16),
                 pltpu.VMEM((d, ff), BF16),
@@ -348,24 +334,41 @@
                 pltpu.VMEM((128, d), F32),
                 pltpu.VMEM((128, d), BF16),
                 pltpu.VMEM((2, 128, d), BF16),
-                pltpu.VMEM((4, 128, half), BF16),
                 pltpu.VMEM((2, 128, d), BF16),
                 pltpu.VMEM((2, 2, 128, half), BF16),
                 pltpu.VMEM((4, 128, half), F32),
                 pltpu.VMEM((2, 2, PIECE, d), BF16),
                 dma((2, 4)), dma((2, 4)), dma((2, 2)), dma((2, 2)), dma((4, 4)), dma((4, 4)),
                 dma((2,)), dma((2,)), dma((2, 4)), dma((2, 4)), dma((2, 2)), dma((2, 2)),
-                dma((2, 4)), dma((2, 4)), dma((2, 2)), dma((3,)), dma((2, 2)), dma((3, 2)),
+                dma((2, 4)), dma((2, 4)), dma((2, 2)), dma((3,)), dma((2, 2)),
             ],
             compiler_params=pltpu.CompilerParams(
-                collective_id=0, has_side_effects=True, vmem_limit_bytes=67043328
+                collective_id=0, has_side_effects=True, vmem_limit_bytes=64487424
             ),
             cost_estimate=pl.CostEstimate(
                 flops=6 * 8 * r * d * ff, bytes_accessed=6 * d * ff + 4 * r * d, transcendentals=8 * r * ff
             ),
             name="mlp",
         )(x, w_gate, w_up, w_down)
-        return y
+        def put(src, dst, sems):
+            out = [
+                pltpu.make_async_copy(src.at[pl.ds(32 * i, 32)], dst.at[pl.ds(32 * i, 32)], sems.at[i])
+                for i in range(8)
+            ]
+            for c in out:
+                c.start()
+            for c in out:
+                c.wait()
+
+        return pl.pallas_call(
+            put,
+            out_shape=jax.ShapeDtypeStruct((r, d), BF16),
+            in_specs=[pl.BlockSpec(memory_space=pltpu.VMEM)],
+            out_specs=hbm,
+            scratch_shapes=[dma((8,))],
+            compiler_params=pltpu.CompilerParams(vmem_limit_bytes=4194304),
+            name="put",
+        )(y)
 
     return jax.shard_map(
         step,

time: 146 us -> 143 us (0.979)
  local copies, waits for them, and re-layouts: 3.13 us -> 0 us
    unnamed x1 -> x0, local copies, waits for them, and re-layouts: 3.13 us -> none
    pallas_call x1 -> x2, Pallas kernels: 142 us -> 143 us  [the longest x1 141 us: step(): pl.pallas_call(body, out_shape=(pltpu.VMEM((r, d), BF16), jax.ShapeDtypeS...]
where the time goes in v4:
time: 143 us
  Pallas kernels  143 us (100%)
    pallas_call x1, Pallas kernels, step(): pl.pallas_call(body, out_shape=(pltpu.VMEM((r, d), BF16), jax.ShapeDtypeS...  141 us

profile of v4, /device:TPU:0, one launch (start us, length us, event | category | flops | bytes accessed | tf_op | source)
XLA Modules:
  0.0 142.8 jit_solution(5694413916336739688)
XLA Ops:
  0.0 141.4 %mlp.1 = (bf16[256,4096]{1,0:T(8,128)(2,1)S(1)}, bf16[4,2,256,4096]{3,2,1,0:T(8,128)(2,1)}, bf16[2,2,64,4096]{3,2,1,0:T(8,128)(2,1)}) custom-call(bf16[256,4096]{1,0:T(8,128)(2,1)} %x.1, bf16[4096,1792]{1,0:T(8,128)(2,1)} %wg_h.1, bf16[4096,1792]{1,0:T(8,128)(2,1)} %wu_h.1, bf16[1792,4096]{1,0:T(8,128)(2,1)} %wd_h.1), custom_call_target="tpu_custom_call" | custom-call | flops 90194313216 | bytes 48234496 | tf_op jit(solution)/shard_map/mlp/pallas_call | solution.py:319
  141.4 1.4 put.1

commit v5 on v4

v5 whole, which is shorter than its diff:
```python
import jax
import jax.numpy as jnp
from jax import lax
from jax.experimental import pallas as pl
from jax.experimental.pallas import tpu as pltpu
from jax.sharding import PartitionSpec as P

F32 = jnp.float32
BF16 = jnp.bfloat16
MESH = pl.DeviceIdType.MESH

SIB, YN, XN = 1, 2, 4
LINK = (XN, YN)
OWN, FX, FY, DG = 0, 1, 2, 3
PIECE = 64
STEPS = 8
X_STEPS = {0: 0, 1: 1, 2: 2, 4: 3}
D_STEPS = {3: 0, 5: 1}
SWAP = (1, 0, 3, 2)
GT = 256
DT = 1024


def body(
    x, wg_h, wu_h, wd_h, y, xg, fh,
    wg, wu, wd, xb, hb, mine, tsend, trecv, outg, rly, hold, fv,
    sent, ro, rr, rs, rt, rg, rf, lx, lw,
):
    me = lax.axis_index("tp")
    d = x.shape[1]
    half = d // 2
    ff = wg.shape[1]
    cols = (pl.ds(0, half), pl.ds(half, half))

    def remote(src, dst, send, recv, mask):
        return pltpu.make_async_remote_copy(
            src_ref=src, dst_ref=dst, send_sem=send, recv_sem=recv,
            device_id={"tp": me ^ mask}, device_id_type=MESH,
        )

    def rows(k, n=1):
        return pl.ds(k * PIECE, n * PIECE)

    def drain(sem, n):
        ref = {1: xg.at[0, 0, rows(0)], 2: xg.at[0, 0, rows(0, 2)], 4: xg.at[0, 0], 32: xg}[n]
        pltpu.make_async_copy(ref, ref, sem).wait()

    def turn(l, k):
        return SWAP[k] if l else k

    def own(l, k):
        n = turn(l, k)
        return remote(x.at[rows(k)], xg.at[FX + l, 0, rows(k)], sent.at[0], ro.at[n], LINK[l])

    def relay(l, r):
        k = 2 * r + 1 - l
        return remote(
            xg.at[FY - l, 0, rows(k)], xg.at[DG, 0, rows(k)], sent.at[0], rr.at[r], LINK[l]
        )

    def hand_own():
        return remote(x, xg.at[OWN, 1], sent.at[0], rs.at[2], SIB)

    def hand(s):
        return [
            remote(xg.at[b, 0, rows(k)], xg.at[b, 1, rows(k)], sent.at[0], rs.at[s % 2], SIB)
            for b, k in pieces(s)
        ]

    def term(s):
        return remote(tsend, trecv.at[s % 2], sent.at[1], rt.at[s % 2], SIB)

    def landing(c):
        return fv if c else fh

    def direct(l, c):
        src = y.at[rows(2 * c, 2), cols[l]]
        return remote(src, landing(c).at[l, :, cols[l]], sent.at[2], rf.at[c], LINK[l])

    def diag(l, c):
        return remote(outg.at[c, :, cols[l]], rly.at[c, l], sent.at[0], rg.at[c], LINK[l])

    def relayed(l, c, k, n, sem):
        dst = landing(c).at[l, rows(k, n), cols[1 - l]]
        return remote(rly.at[c, 1 - l, rows(k, n)], dst, sent.at[3], rf.at[sem], LINK[l])

    RELAYED = (((0, 2, 0),), ((0, 1, 2), (1, 1, 3)))

    def pieces(s):
        if s in X_STEPS:
            return tuple((FX + l, turn(l, X_STEPS[s])) for l in range(2))
        b, c = (DG, D_STEPS[s]) if s in D_STEPS else (OWN, s - 6)
        return ((b, 2 * c), (b, 2 * c + 1))

    def load(s, side):
        out = []
        for i, (b, k) in enumerate(pieces(s)):
            src = x.at[rows(k)] if (b == OWN and side == 0) else xg.at[b, side, rows(k)]
            out.append(pltpu.make_async_copy(src, xb.at[rows(2 * side + i)], lx.at[0]))
        return out

    def take(s):
        if s in X_STEPS:
            drain(ro.at[X_STEPS[s]], 2)
        elif s in D_STEPS:
            drain(rr.at[D_STEPS[s]], 2)
        if s < 6:
            for c in hand(s):
                c.start()
        for c in load(s, 0):
            c.start()
        if s == 1:
            for l in range(2):
                relay(l, 0).start()
                own(l, turn(l, 3)).start()
        if s == 2:
            for l in range(2):
                relay(l, 1).start()

    def take_other(s):
        if s < 6:
            drain(rs.at[s % 2], 2)
        elif s == 6:
            hand_own().wait_recv()
        for c in load(s, 1):
            c.start()

    weights = [
        pltpu.make_async_copy(h, v, lw.at[i])
        for i, (h, v) in enumerate(((wg_h, wg), (wu_h, wu), (wd_h, wd)))
    ]

    def total(r, slot):
        return mine[r] + trecv[slot, r].astype(F32)

    def blocks(n, f):
        def one(i, carry):
            f(pl.multiple_of(i * 16, 16))
            return carry

        lax.fori_loop(0, n, one, 0)

    def settle(p):
        slot = p % 2
        term(p).wait_recv()
        if p in X_STEPS:
            n = X_STEPS[p]
            for l in range(2):

                def f(i, l=l):
                    v = total(pl.ds(l * PIECE + i, 16), slot)
                    a, b = v[:, :half], v[:, half:]
                    r = pl.ds(turn(l, n) * PIECE + i, 16)
                    y[r, cols[l]] = (b if l else a).astype(BF16)
                    hold[l, r] = a if l else b

                blocks(PIECE // 16, f)
            if n % 2:
                for l in range(2):
                    direct(l, n // 2).start()
        elif p in D_STEPS:
            n = D_STEPS[p]

            def f(i):
                r = pl.ds(i, 16)
                outg[n, r] = total(r, slot).astype(BF16)

            blocks(8, f)
            for l in range(2):
                diag(l, n).start()
        else:

            def f(i):
                r = pl.ds(i, 16)
                v = total(r, slot)
                hold[0, r] = v[:, :half]
                hold[1, r] = v[:, half:]

            blocks(8, f)

    def pass_on(c):
        drain(rg.at[c], 2)
        for k, n, sem in RELAYED[c]:
            for l in range(2):

                def f(i, k=k, l=l):
                    r = pl.ds(k * PIECE + i, 16)
                    v = hold[l, pl.ds((2 * c + k) * PIECE + i, 16)] + rly[c, 1 - l, r].astype(F32)
                    rly[c, 1 - l, r] = v.astype(BF16)

                blocks(n * PIECE // 16, f)
                relayed(l, c, k, n, sem).start()

    def gate_up(lo, hi):
        def one(j, carry):
            c = pl.ds(pl.multiple_of(j * GT, GT), GT)
            g = jnp.dot(xb[...], wg[:, c], preferred_element_type=F32)
            u = jnp.dot(xb[...], wu[:, c], preferred_element_type=F32)
            hb[:, c] = (jax.nn.silu(g) * u).astype(BF16)
            return carry

        lax.fori_loop(lo, hi, one, 0, unroll=True)

    def down(lo, hi):
        def one(j, carry):
            c = pl.ds(pl.multiple_of(j * DT, DT), DT)
            t = jnp.dot(hb[...], wd[:, c], preferred_element_type=F32)
            mine[:, c] = t[: 2 * PIECE]
            tsend[:, c] = t[2 * PIECE :].astype(BF16)
            return carry

        lax.fori_loop(lo, hi, one, 0, unroll=True)

    barrier = pltpu.get_barrier_semaphore()
    for mask in (SIB, YN, XN):
        pl.semaphore_signal(barrier, inc=1, device_id={"tp": me ^ mask}, device_id_type=MESH)
    pl.semaphore_wait(barrier, 3)

    for k in range(3):
        for l in range(2):
            own(l, turn(l, k)).start()
    for i in range(2):
        weights[i].start()
    for i in range(2):
        weights[i].wait()
    weights[2].start()
    take(0)
    take_other(0)
    hand_own().start()

    def at(s, table):
        for k, fs in table.items():

            @pl.when(s == k)
            def _(fs=fs):
                for f, *args in fs:
                    f(*args)

    after_tiles = {p + 1: [(settle, p)] for p in range(7)}
    after_gate = {s: [(take, s + 1)] for s in range(7)}
    late = {s: [(take_other, s + 1)] for s in range(7)}
    ends = {s: [(term(s).start,)] for s in range(STEPS)}
    after_gate[7] = []
    after_gate[0].append((weights[2].wait,))
    after_gate[6].append((pass_on, 0))
    ends[7].append((pass_on, 1))
    for s in range(1, STEPS):
        after_gate[s].append((term(s - 1).wait_send,))

    def step(s, carry):
        drain(lx.at[0], 4)
        gate_up(0, 3)
        at(s, after_tiles)
        gate_up(3, ff // GT)
        at(s, after_gate)
        down(0, d // DT - 1)
        at(s, late)
        down(d // DT - 1, d // DT)
        at(s, ends)
        return carry

    lax.fori_loop(0, STEPS, step, 0)

    drain(sent.at[2], 4)
    drain(rf.at[0], 4)
    back = [pltpu.make_async_copy(fh.at[l], xb.at[rows(2 * l, 2)], lx.at[0]) for l in range(2)]
    for c in back:
        c.start()
    drain(lx.at[0], 4)

    def first(i):
        r = pl.ds(i, 16)
        v = xb[r].astype(F32) + xb[pl.ds(2 * PIECE + i, 16)].astype(F32)
        y[r, cols[0]] = (hold[0, r] + v[:, :half]).astype(BF16)
        y[r, cols[1]] = (hold[1, r] + v[:, half:]).astype(BF16)

    blocks(2 * PIECE // 16, first)
    term(7).wait_recv()
    drain(rf.at[1], 2)

    def add_direct(i):
        r = pl.ds(i, 16)
        for c, l in zip(cols, range(2)):
            mine[r, c] += trecv[1, r, c].astype(F32) + fv[l, r, c].astype(F32)

    blocks(2 * PIECE // 16, add_direct)
    for k, n, sem in RELAYED[1]:
        drain(rf.at[sem], 1)

        def add_relayed(i, k=k):
            r = pl.ds(k * PIECE + i, 16)
            for c, l in zip(cols, range(2)):
                v = mine[r, c] + fv[1 - l, r, c].astype(F32)
                y[pl.ds((2 + k) * PIECE + i, 16), c] = v.astype(BF16)

        blocks(n * PIECE // 16, add_relayed)
    term(7).wait_send()
    drain(sent.at[0], 32)
    drain(sent.at[3], 4)


def solution(mesh):
    def step(x, w_gate, w_up, w_down):
        r, d = x.shape
        ff = w_gate.shape[1]
        hbm = pl.BlockSpec(memory_space=pl.ANY)
        dma = pltpu.SemaphoreType.DMA
        half = d // 2
        y, _, _ = pl.pallas_call(
            body,
            out_shape=(
                pltpu.VMEM((r, d), BF16),
                jax.ShapeDtypeStruct((4, 2, r, d), BF16),
                jax.ShapeDtypeStruct((2, 2 * PIECE, d), BF16),
            ),
            in_specs=[hbm] * 4,
            out_specs=(pl.BlockSpec(memory_space=pltpu.VMEM), hbm, hbm),
            scratch_shapes=[
                pltpu.VMEM((d, ff), BF16),
                pltpu.VMEM((d, ff), BF16),
                pltpu.VMEM((ff, d), BF16),
                pltpu.VMEM((256, d), BF16),
                pltpu.VMEM((256, ff), BF16),
                pltpu.VMEM((128, d), F32),
                pltpu.VMEM((128, d), BF16),
                pltpu.VMEM((2, 128, d), BF16),
                pltpu.VMEM((2, 128, d), BF16),
                pltpu.VMEM((2, 2, 128, half), BF16),
                pltpu.VMEM((2, 256, half), F32),
                pltpu.VMEM((2, 2 * PIECE, d), BF16),
                dma((4,)), dma((4,)), dma((2,)), dma((3,)), dma((2,)), dma((2,)), dma((4,)), dma((1,)), dma((3,)),
            ],
            compiler_params=pltpu.CompilerParams(
                collective_id=0, has_side_effects=True, vmem_limit_bytes=64487424
            ),
            cost_estimate=pl.CostEstimate(
                flops=6 * 8 * r * d * ff, bytes_accessed=6 * d * ff + 4 * r * d, transcendentals=8 * r * ff
            ),
            name="mlp",
        )(x, w_gate, w_up, w_down)
        def put(src, dst, sem):
            c = pltpu.make_async_copy(src, dst, sem.at[0])
            c.start()
            c.wait()

        return pl.pallas_call(
            put,
            out_shape=jax.ShapeDtypeStruct((r, d), BF16),
            in_specs=[pl.BlockSpec(memory_space=pltpu.VMEM)],
            out_specs=hbm,
            scratch_shapes=[dma((1,))],
            compiler_params=pltpu.CompilerParams(vmem_limit_bytes=4194304),
            name="put",
        )(y)

    return jax.shard_map(
        step,
        mesh=mesh,
        in_specs=(P(("dp", "tp"), None), P(None, "tp"), P(None, "tp"), P("tp", None)),
        out_specs=P(("dp", "tp"), None),
        check_vma=False,
    )
```

time: 143 us -> 142 us (level)
  no operation moved by 1% of the time
where the time goes in v5:
time: 142 us
  Pallas kernels  142 us (100%)
    pallas_call x1, Pallas kernels, step(): pl.pallas_call(body, out_shape=(pltpu.VMEM((r, d), BF16), jax.ShapeDtypeS...  140 us

profile of v5, /device:TPU:0, one launch (start us, length us, event | category | flops | bytes accessed | tf_op | source)
XLA Modules:
  0.0 141.8 jit_solution(4870539893884021717)
XLA Ops:
  0.0 140.4 %mlp.1 = (bf16[256,4096]{1,0:T(8,128)(2,1)S(1)}, bf16[4,2,256,4096]{3,2,1,0:T(8,128)(2,1)}, bf16[2,128,4096]{2,1,0:T(8,128)(2,1)}) custom-call(bf16[256,4096]{1,0:T(8,128)(2,1)} %x.1, bf16[4096,1792]{1,0:T(8,128)(2,1)} %wg_h.1, bf16[4096,1792]{1,0:T(8,128)(2,1)} %wu_h.1, bf16[1792,4096]{1,0:T(8,128)(2,1)} %wd_h.1), custom_call_target="tpu_custom_call" | custom-call | flops 90194313216 | bytes 48234496 | tf_op jit(solution)/shard_map/mlp/pallas_call | solution.py:309
  140.4 1.3 put.1

commit v6 on v5

--- a/solution.py
+++ b/solution.py
@@ -24,7 +24,7 @@
 def body(
     x, wg_h, wu_h, wd_h, y, xg, fh,
     wg, wu, wd, xb, hb, mine, tsend, trecv, outg, rly, hold, fv,
-    sent, ro, rr, rs, rt, rg, rf, lx, lw,
+    sent, ro, rr, rs, rt, rg, rf, lx, lw, late,
 ):
     me = lax.axis_index("tp")
     d = x.shape[1]
@@ -211,16 +211,53 @@
 
         lax.fori_loop(lo, hi, one, 0, unroll=True)
 
+    chip = me // 2
+    middle = (chip == 1) | (chip == 2)
     barrier = pltpu.get_barrier_semaphore()
-    for mask in (SIB, YN, XN):
-        pl.semaphore_signal(barrier, inc=1, device_id={"tp": me ^ mask}, device_id_type=MESH)
-    pl.semaphore_wait(barrier, 3)
-
-    for k in range(3):
-        for l in range(2):
+
+    def greet(sem, mask):
+        pl.semaphore_signal(sem, inc=1, device_id={"tp": me ^ mask}, device_id_type=MESH)
+
+    greet(barrier, SIB)
+
+    @pl.when(chip != 3)
+    def _():
+        for mask in LINK:
+            greet(barrier, mask)
+
+    @pl.when(middle)
+    def _():
+        pl.semaphore_wait(barrier, 2)
+
+    @pl.when(jnp.logical_not(middle))
+    def _():
+        pl.semaphore_wait(barrier, 3)
+
+    @pl.when(chip == 3)
+    def _():
+        for mask in LINK:
+            greet(late, mask)
+
+    def first_pieces(l):
+        for k in range(3):
             own(l, turn(l, k)).start()
+
+    to_last = [chip ^ (LINK[l] // 2) == 3 for l in range(2)]
+    for l in range(2):
+
+        @pl.when(jnp.logical_not(to_last[l]))
+        def _(l=l):
+            first_pieces(l)
+
     for i in range(2):
         weights[i].start()
+    for l in range(2):
+
+        @pl.when(to_last[l])
+        def _(l=l):
+            pl.semaphore_wait(late, 1)
+            first_pieces(l)
+
     for i in range(2):
         weights[i].wait()
     weights[2].start()
@@ -238,7 +275,7 @@
 
     after_tiles = {p + 1: [(settle, p)] for p in range(7)}
     after_gate = {s: [(take, s + 1)] for s in range(7)}
-    late = {s: [(take_other, s + 1)] for s in range(7)}
+    after_tile = {s: [(take_other, s + 1)] for s in range(7)}
     ends = {s: [(term(s).start,)] for s in range(STEPS)}
     after_gate[7] = []
     after_gate[0].append((weights[2].wait,))
@@ -254,7 +291,7 @@
         gate_up(3, ff // GT)
         at(s, after_gate)
         down(0, d // DT - 1)
-        at(s, late)
+        at(s, after_tile)
         down(d // DT - 1, d // DT)
         at(s, ends)
         return carry
@@ -329,6 +366,7 @@
                 pltpu.VMEM((2, 256, half), F32),
                 pltpu.VMEM((2, 2 * PIECE, d), BF16),
                 dma((4,)), dma((4,)), dma((2,)), dma((3,)), dma((2,)), dma((2,)), dma((4,)), dma((1,)), dma((3,)),
+                pltpu.SemaphoreType.REGULAR,
             ],
             compiler_params=pltpu.CompilerParams(
                 collective_id=0, has_side_effects=True, vmem_limit_bytes=64487424

time: 142 us -> 142 us (level)
  no operation moved by 1% of the time
where the time goes in v6:
time: 142 us; the launch traced here: 141 us
  Pallas kernels  141 us (99%)
    pallas_call x1, Pallas kernels, step(): pl.pallas_call(body, out_shape=(pltpu.VMEM((r, d), BF16), jax.ShapeDtypeS...  140 us

profile of v6, /device:TPU:0, one launch (start us, length us, event | category | flops | bytes accessed | tf_op | source)
XLA Modules:
  0.0 141.2 jit_solution(11654664135002140415)
XLA Ops:
  0.0 139.9 %mlp.1 = (bf16[256,4096]{1,0:T(8,128)(2,1)S(1)}, bf16[4,2,256,4096]{3,2,1,0:T(8,128)(2,1)}, bf16[2,128,4096]{2,1,0:T(8,128)(2,1)}) custom-call(bf16[256,4096]{1,0:T(8,128)(2,1)} %x.1, bf16[4096,1792]{1,0:T(8,128)(2,1)} %wg_h.1, bf16[4096,1792]{1,0:T(8,128)(2,1)} %wu_h.1, bf16[1792,4096]{1,0:T(8,128)(2,1)} %wd_h.1), custom_call_target="tpu_custom_call" | custom-call | flops 90194313216 | bytes 48234496 | tf_op jit(solution)/shard_map/mlp/pallas_call | solution.py:346
  139.9 1.3 put.1

commit v7 on v6

--- a/solution.py
+++ b/solution.py
@@ -243,19 +243,24 @@
             own(l, turn(l, k)).start()
 
     to_last = [chip ^ (LINK[l] // 2) == 3 for l in range(2)]
+    behind = middle & (me % 2 == 1)
     for l in range(2):
 
-        @pl.when(jnp.logical_not(to_last[l]))
+        @pl.when(jnp.logical_not(to_last[l] | behind))
         def _(l=l):
             first_pieces(l)
 
     for i in range(2):
         weights[i].start()
+
+    @pl.when(middle)
+    def _():
+        pl.semaphore_wait(late, 1)
+
     for l in range(2):
 
-        @pl.when(to_last[l])
+        @pl.when(to_last[l] | behind)
         def _(l=l):
-            pl.semaphore_wait(late, 1)
             first_pieces(l)
 
     for i in range(2):

time: 142 us -> 141 us (level)
  no operation moved by 1% of the time
where the time goes in v7:
time: 141 us; the launch traced here: 140 us
  Pallas kernels  140 us (99%)
    pallas_call x1, Pallas kernels, step(): pl.pallas_call(body, out_shape=(pltpu.VMEM((r, d), BF16), jax.ShapeDtypeS...  139 us

profile of v7, /device:TPU:0, one launch (start us, length us, event | category | flops | bytes accessed | tf_op | source)
XLA Modules:
  0.0 140.4 jit_solution(2548624201733357094)
XLA Ops:
  0.0 139.0 %mlp.1 = (bf16[256,4096]{1,0:T(8,128)(2,1)S(1)}, bf16[4,2,256,4096]{3,2,1,0:T(8,128)(2,1)}, bf16[2,128,4096]{2,1,0:T(8,128)(2,1)}) custom-call(bf16[256,4096]{1,0:T(8,128)(2,1)} %x.1, bf16[4096,1792]{1,0:T(8,128)(2,1)} %wg_h.1, bf16[4096,1792]{1,0:T(8,128)(2,1)} %wu_h.1, bf16[1792,4096]{1,0:T(8,128)(2,1)} %wd_h.1), custom_call_target="tpu_custom_call" | custom-call | flops 90194313216 | bytes 48234496 | tf_op jit(solution)/shard_map/mlp/pallas_call | solution.py:351
  139.1 1.3 put.1

commit v8 on v5

--- a/solution.py
+++ b/solution.py
@@ -13,6 +13,7 @@
 LINK = (XN, YN)
 OWN, FX, FY, DG = 0, 1, 2, 3
 PIECE = 64
+FEW = 16
 STEPS = 8
 X_STEPS = {0: 0, 1: 1, 2: 2, 4: 3}
 D_STEPS = {3: 0, 5: 1}
@@ -24,7 +25,7 @@
 def body(
     x, wg_h, wu_h, wd_h, y, xg, fh,
     wg, wu, wd, xb, hb, mine, tsend, trecv, outg, rly, hold, fv,
-    sent, ro, rr, rs, rt, rg, rf, lx, lw,
+    sent, ro, rr, rs, rt, rg, rf, lx, lw, late,
 ):
     me = lax.axis_index("tp")
     d = x.shape[1]
@@ -48,9 +49,9 @@
     def turn(l, k):
         return SWAP[k] if l else k
 
-    def own(l, k):
-        n = turn(l, k)
-        return remote(x.at[rows(k)], xg.at[FX + l, 0, rows(k)], sent.at[0], ro.at[n], LINK[l])
+    def own(l, k, lo=0, hi=PIECE):
+        r = pl.ds(k * PIECE + lo, hi - lo)
+        return remote(x.at[r], xg.at[FX + l, 0, r], sent.at[0], ro.at[turn(l, k)], LINK[l])
 
     def relay(l, r):
         k = 2 * r + 1 - l
@@ -211,18 +212,49 @@
 
         lax.fori_loop(lo, hi, one, 0, unroll=True)
 
+    chip = me // 2
+    middle = (chip == 1) | (chip == 2)
+    lead, behind = middle & (me % 2 == 0), middle & (me % 2 == 1)
+    to_last = [chip ^ (LINK[l] // 2) == 3 for l in range(2)]
     barrier = pltpu.get_barrier_semaphore()
-    for mask in (SIB, YN, XN):
-        pl.semaphore_signal(barrier, inc=1, device_id={"tp": me ^ mask}, device_id_type=MESH)
-    pl.semaphore_wait(barrier, 3)
-
-    for k in range(3):
-        for l in range(2):
+
+    def greet(sem, masks):
+        for mask in masks:
+            pl.semaphore_signal(sem, inc=1, device_id={"tp": me ^ mask}, device_id_type=MESH)
+
+    def when(p, f, *args):
+        @pl.when(p)
+        def _():
+            f(*args)
+
+    def first_rows(l):
+        own(l, turn(l, 0), 0, FEW).start()
+
+    def pieces_after(l, lo):
+        own(l, turn(l, 0), lo, PIECE).start()
+        for k in (1, 2):
             own(l, turn(l, k)).start()
+
+    when(jnp.logical_not(lead), greet, barrier, (SIB,))
+    when(chip != 3, greet, barrier, LINK)
+    when(behind, pl.semaphore_wait, barrier, 1)
+    when(lead, pl.semaphore_wait, barrier, 2)
+    when(jnp.logical_not(middle), pl.semaphore_wait, barrier, 3)
+    for l in range(2):
+        when(behind & jnp.logical_not(to_last[l]), first_rows, l)
+        when(jnp.logical_not(behind | to_last[l]), pieces_after, l, 0)
+    when(lead, greet, late, (SIB,))
+    when(chip == 3, greet, late, LINK)
     for i in range(2):
         weights[i].start()
-    for i in range(2):
-        weights[i].wait()
+    when(lead, pl.semaphore_wait, late, 1)
+    when(behind, pl.semaphore_wait, late, 2)
+    for l in range(2):
+        when(to_last[l], pieces_after, l, 0)
+    weights[0].wait()
+    for l in range(2):
+        when(behind & jnp.logical_not(to_last[l]), pieces_after, l, FEW)
+    weights[1].wait()
     weights[2].start()
     take(0)
     take_other(0)
@@ -238,7 +270,7 @@
 
     after_tiles = {p + 1: [(settle, p)] for p in range(7)}
     after_gate = {s: [(take, s + 1)] for s in range(7)}
-    late = {s: [(take_other, s + 1)] for s in range(7)}
+    after_tile = {s: [(take_other, s + 1)] for s in range(7)}
     ends = {s: [(term(s).start,)] for s in range(STEPS)}
     after_gate[7] = []
     after_gate[0].append((weights[2].wait,))
@@ -254,7 +286,7 @@
         gate_up(3, ff // GT)
         at(s, after_gate)
         down(0, d // DT - 1)
-        at(s, late)
+        at(s, after_tile)
         down(d // DT - 1, d // DT)
         at(s, ends)
         return carry
@@ -329,6 +361,7 @@
                 pltpu.VMEM((2, 256, half), F32),
                 pltpu.VMEM((2, 2 * PIECE, d), BF16),
                 dma((4,)), dma((4,)), dma((2,)), dma((3,)), dma((2,)), dma((2,)), dma((4,)), dma((1,)), dma((3,)),
+                pltpu.SemaphoreType.REGULAR,
             ],
             compiler_params=pltpu.CompilerParams(
                 collective_id=0, has_side_effects=True, vmem_limit_bytes=64487424
@@ -343,15 +376,7 @@
             c.start()
             c.wait()
 
-        return pl.pallas_call(
-            put,
-            out_shape=jax.ShapeDtypeStruct((r, d), BF16),
-            in_specs=[pl.BlockSpec(memory_space=pltpu.VMEM)],
-            out_specs=hbm,
-            scratch_shapes=[dma((1,))],
-            compiler_params=pltpu.CompilerParams(vmem_limit_bytes=4194304),
-            name="put",
-        )(y)
+        return y
 
     return jax.shard_map(
         step,

time: 142 us -> 140 us (0.986)
  Pallas kernels: 142 us -> 138 us
    pallas_call x1, Pallas kernels: 140 us -> 138 us  [step(): pl.pallas_call(body, out_shape=(pltpu.VMEM((r, d), BF16), jax.ShapeDtypeS...]
where the time goes in v8:
time: 140 us
  Pallas kernels  138 us (99%)
    pallas_call x1, Pallas kernels, step(): pl.pallas_call(body, out_shape=(pltpu.VMEM((r, d), BF16), jax.ShapeDtypeS...  138 us

profile of v8, /device:TPU:0, one launch (start us, length us, event | category | flops | bytes accessed | tf_op | source)
XLA Modules:
  0.0 139.7 jit_solution(6257361802217972983)
XLA Ops:
  0.0 138.4 %mlp.1 = (bf16[256,4096]{1,0:T(8,128)(2,1)S(1)}, bf16[4,2,256,4096]{3,2,1,0:T(8,128)(2,1)}, bf16[2,128,4096]{2,1,0:T(8,128)(2,1)}) custom-call(bf16[256,4096]{1,0:T(8,128)(2,1)} %x.1, bf16[4096,1792]{1,0:T(8,128)(2,1)} %wg_h.1, bf16[4096,1792]{1,0:T(8,128)(2,1)} %wu_h.1, bf16[1792,4096]{1,0:T(8,128)(2,1)} %wd_h.1), custom_call_target="tpu_custom_call" | custom-call | flops 90194313216 | bytes 48234496 | tf_op jit(solution)/shard_map/mlp/pallas_call | solution.py:341
  138.4 1.3 copy.6

commit v9 on v8

--- a/solution.py
+++ b/solution.py
@@ -215,6 +215,8 @@
     chip = me // 2
     middle = (chip == 1) | (chip == 2)
     lead, behind = middle & (me % 2 == 0), middle & (me % 2 == 1)
+    last0, last1 = (chip == 3) & (me % 2 == 0), (chip == 3) & (me % 2 == 1)
+    slow = (chip == 0) & (me % 2 == 1)
     to_last = [chip ^ (LINK[l] // 2) == 3 for l in range(2)]
     barrier = pltpu.get_barrier_semaphore()
 
@@ -235,25 +237,26 @@
         for k in (1, 2):
             own(l, turn(l, k)).start()
 
-    when(jnp.logical_not(lead), greet, barrier, (SIB,))
+    when(jnp.logical_not(lead | last0), greet, barrier, (SIB,))
     when(chip != 3, greet, barrier, LINK)
     when(behind, pl.semaphore_wait, barrier, 1)
     when(lead, pl.semaphore_wait, barrier, 2)
-    when(jnp.logical_not(middle), pl.semaphore_wait, barrier, 3)
+    when(last1, pl.semaphore_wait, barrier, 2)
+    when(jnp.logical_not(middle | last1), pl.semaphore_wait, barrier, 3)
     for l in range(2):
-        when(behind & jnp.logical_not(to_last[l]), first_rows, l)
-        when(jnp.logical_not(behind | to_last[l]), pieces_after, l, 0)
-    when(lead, greet, late, (SIB,))
+        when((behind & jnp.logical_not(to_last[l])) | slow, first_rows, l)
+        when(jnp.logical_not(behind | to_last[l] | slow), pieces_after, l, 0)
+    when(lead | last0, greet, late, (SIB,))
     when(chip == 3, greet, late, LINK)
     for i in range(2):
         weights[i].start()
-    when(lead, pl.semaphore_wait, late, 1)
+    when(lead | last1, pl.semaphore_wait, late, 1)
     when(behind, pl.semaphore_wait, late, 2)
     for l in range(2):
         when(to_last[l], pieces_after, l, 0)
     weights[0].wait()
     for l in range(2):
-        when(behind & jnp.logical_not(to_last[l]), pieces_after, l, FEW)
+        when((behind & jnp.logical_not(to_last[l])) | slow, pieces_after, l, FEW)
     weights[1].wait()
     weights[2].start()
     take(0)

time: 140 us -> 140 us (level)
  no operation moved by 1% of the time
where the time goes in v9:
time: 140 us; the launch traced here: 138 us
  Pallas kernels  137 us (98%)
    pallas_call x1, Pallas kernels, step(): pl.pallas_call(body, out_shape=(pltpu.VMEM((r, d), BF16), jax.ShapeDtypeS...  137 us

profile of v9, /device:TPU:0, one launch (start us, length us, event | category | flops | bytes accessed | tf_op | source)
XLA Modules:
  0.0 138.4 jit_solution(18172532035125797195)
XLA Ops:
  0.0 137.1 %mlp.1 = (bf16[256,4096]{1,0:T(8,128)(2,1)S(1)}, bf16[4,2,256,4096]{3,2,1,0:T(8,128)(2,1)}, bf16[2,128,4096]{2,1,0:T(8,128)(2,1)}) custom-call(bf16[256,4096]{1,0:T(8,128)(2,1)} %x.1, bf16[4096,1792]{1,0:T(8,128)(2,1)} %wg_h.1, bf16[4096,1792]{1,0:T(8,128)(2,1)} %wu_h.1, bf16[1792,4096]{1,0:T(8,128)(2,1)} %wd_h.1), custom_call_target="tpu_custom_call" | custom-call | flops 90194313216 | bytes 48234496 | tf_op jit(solution)/shard_map/mlp/pallas_call | solution.py:344
  137.1 1.3 copy.6

commit v10 on v9

--- a/solution.py
+++ b/solution.py
@@ -25,7 +25,7 @@
 def body(
     x, wg_h, wu_h, wd_h, y, xg, fh,
     wg, wu, wd, xb, hb, mine, tsend, trecv, outg, rly, hold, fv,
-    sent, ro, rr, rs, rt, rg, rf, lx, lw, late,
+    sent, ro, rr, rs, rt, rf, lx, lw, late,
 ):
     me = lax.axis_index("tp")
     d = x.shape[1]
@@ -46,6 +46,8 @@
         ref = {1: xg.at[0, 0, rows(0)], 2: xg.at[0, 0, rows(0, 2)], 4: xg.at[0, 0], 32: xg}[n]
         pltpu.make_async_copy(ref, ref, sem).wait()
 
+    last_sem = (rf.at[0], ro.at[2], ro.at[3], rr.at[0])
+
     def turn(l, k):
         return SWAP[k] if l else k
 
@@ -76,14 +78,14 @@
 
     def direct(l, c):
         src = y.at[rows(2 * c, 2), cols[l]]
-        return remote(src, landing(c).at[l, :, cols[l]], sent.at[2], rf.at[c], LINK[l])
+        return remote(src, landing(c).at[l, :, cols[l]], sent.at[2], last_sem[c], LINK[l])
 
     def diag(l, c):
-        return remote(outg.at[c, :, cols[l]], rly.at[c, l], sent.at[0], rg.at[c], LINK[l])
+        return remote(outg.at[c, :, cols[l]], rly.at[c, l], sent.at[0], ro.at[c], LINK[l])
 
     def relayed(l, c, k, n, sem):
         dst = landing(c).at[l, rows(k, n), cols[1 - l]]
-        return remote(rly.at[c, 1 - l, rows(k, n)], dst, sent.at[3], rf.at[sem], LINK[l])
+        return remote(rly.at[c, 1 - l, rows(k, n)], dst, sent.at[3], last_sem[sem], LINK[l])
 
     RELAYED = (((0, 2, 0),), ((0, 1, 2), (1, 1, 3)))
 
@@ -127,7 +129,7 @@
             c.start()
 
     weights = [
-        pltpu.make_async_copy(h, v, lw.at[i])
+        pltpu.make_async_copy(h, v, lw.at[0] if i else lx.at[0])
         for i, (h, v) in enumerate(((wg_h, wg), (wu_h, wu), (wd_h, wd)))
     ]
 
@@ -180,7 +182,7 @@
             blocks(8, f)
 
     def pass_on(c):
-        drain(rg.at[c], 2)
+        drain(ro.at[c], 2)
         for k, n, sem in RELAYED[c]:
             for l in range(2):
 
@@ -311,7 +313,7 @@
 
     blocks(2 * PIECE // 16, first)
     term(7).wait_recv()
-    drain(rf.at[1], 2)
+    drain(last_sem[1], 2)
 
     def add_direct(i):
         r = pl.ds(i, 16)
@@ -320,7 +322,7 @@
 
     blocks(2 * PIECE // 16, add_direct)
     for k, n, sem in RELAYED[1]:
-        drain(rf.at[sem], 1)
+        drain(last_sem[sem], 1)
 
         def add_relayed(i, k=k):
             r = pl.ds(k * PIECE + i, 16)
@@ -363,7 +365,7 @@
                 pltpu.VMEM((2, 2, 128, half), BF16),
                 pltpu.VMEM((2, 256, half), F32),
                 pltpu.VMEM((2, 2 * PIECE, d), BF16),
-                dma((4,)), dma((4,)), dma((2,)), dma((3,)), dma((2,)), dma((2,)), dma((4,)), dma((1,)), dma((3,)),
+                dma((4,)), dma((4,)), dma((2,)), dma((3,)), dma((2,)), dma((1,)), dma((1,)), dma((1,)),
                 pltpu.SemaphoreType.REGULAR,
             ],
             compiler_params=pltpu.CompilerParams(

time: 140 us -> 140 us (level)
  no operation moved by 1% of the time
where the time goes in v10:
time: 140 us; the launch traced here: 138 us
  Pallas kernels  137 us (98%)
    pallas_call x1, Pallas kernels, step(): pl.pallas_call(body, out_shape=(pltpu.VMEM((r, d), BF16), jax.ShapeDtypeS...  137 us

profile of v10, /device:TPU:0, one launch (start us, length us, event | category | flops | bytes accessed | tf_op | source)
XLA Modules:
  0.0 138.3 jit_solution(2601692267866199174)
XLA Ops:
  0.0 137.0 %mlp.1 = (bf16[256,4096]{1,0:T(8,128)(2,1)S(1)}, bf16[4,2,256,4096]{3,2,1,0:T(8,128)(2,1)}, bf16[2,128,4096]{2,1,0:T(8,128)(2,1)}) custom-call(bf16[256,4096]{1,0:T(8,128)(2,1)} %x.1, bf16[4096,1792]{1,0:T(8,128)(2,1)} %wg_h.1, bf16[4096,1792]{1,0:T(8,128)(2,1)} %wu_h.1, bf16[1792,4096]{1,0:T(8,128)(2,1)} %wd_h.1), custom_call_target="tpu_custom_call" | custom-call | flops 90194313216 | bytes 48234496 | tf_op jit(solution)/shard_map/mlp/pallas_call | solution.py:346
  137.0 1.3 copy.6

commit v11 on v10

--- a/solution.py
+++ b/solution.py
@@ -25,7 +25,7 @@
 def body(
     x, wg_h, wu_h, wd_h, y, xg, fh,
     wg, wu, wd, xb, hb, mine, tsend, trecv, outg, rly, hold, fv,
-    sent, ro, rr, rs, rt, rf, lx, lw, late,
+    sent, ro, rr, rs, rt, rf, lx, late,
 ):
     me = lax.axis_index("tp")
     d = x.shape[1]
@@ -129,7 +129,7 @@
             c.start()
 
     weights = [
-        pltpu.make_async_copy(h, v, lw.at[0] if i else lx.at[0])
+        pltpu.make_async_copy(h, v, (lx.at[0], rt.at[0], rt.at[1])[i])
         for i, (h, v) in enumerate(((wg_h, wg), (wu_h, wu), (wd_h, wd)))
     ]
 
@@ -365,7 +365,7 @@
                 pltpu.VMEM((2, 2, 128, half), BF16),
                 pltpu.VMEM((2, 256, half), F32),
                 pltpu.VMEM((2, 2 * PIECE, d), BF16),
-                dma((4,)), dma((4,)), dma((2,)), dma((3,)), dma((2,)), dma((1,)), dma((1,)), dma((1,)),
+                dma((4,)), dma((4,)), dma((2,)), dma((3,)), dma((2,)), dma((1,)), dma((1,)),
                 pltpu.SemaphoreType.REGULAR,
             ],
             compiler_params=pltpu.CompilerParams(

time: 140 us -> 140 us (level)
  no operation moved by 1% of the time
where the time goes in v11:
time: 140 us; the launch traced here: 138 us
  Pallas kernels  137 us (98%)
    pallas_call x1, Pallas kernels, step(): pl.pallas_call(body, out_shape=(pltpu.VMEM((r, d), BF16), jax.ShapeDtypeS...  137 us

profile of v11, /device:TPU:0, one launch (start us, length us, event | category | flops | bytes accessed | tf_op | source)
XLA Modules:
  0.0 138.3 jit_solution(1177591197437330586)
XLA Ops:
  0.0 137.0 %mlp.1 = (bf16[256,4096]{1,0:T(8,128)(2,1)S(1)}, bf16[4,2,256,4096]{3,2,1,0:T(8,128)(2,1)}, bf16[2,128,4096]{2,1,0:T(8,128)(2,1)}) custom-call(bf16[256,4096]{1,0:T(8,128)(2,1)} %x.1, bf16[4096,1792]{1,0:T(8,128)(2,1)} %wg_h.1, bf16[4096,1792]{1,0:T(8,128)(2,1)} %wu_h.1, bf16[1792,4096]{1,0:T(8,128)(2,1)} %wd_h.1), custom_call_target="tpu_custom_call" | custom-call | flops 90194313216 | bytes 48234496 | tf_op jit(solution)/shard_map/mlp/pallas_call | solution.py:346
  137.0 1.3 copy.6
